TPU v7x, 128 devices: a whole 4x4x4 slice. The times are simulated.
128 devices in a mesh: row: 8 (over y, z_lo), col: 16 (over x, z_hi, core).
Axes of the slice: x: 4, y: 4, z: 4 (z_hi: 2, z_lo: 2; z = z_hi * 2 + z_lo), core: 2. Of those that a mesh axis runs over, the one named last changes fastest.
Arguments:
- hidden_states: bfloat16 [16384, 8192], P(('row', 'col')), may hold values from -6 to 6
- w_c: bfloat16 [8192, 512], replicated, may hold values from -0.0625 to 0.0625
- w_b: bfloat16 [8192, 128], replicated, may hold values from -0.0625 to 0.0625
- teacher_q: bfloat16 [16384, 512], P(('row', 'col')), may hold values from -4 to 4
- teacher_k: bfloat16 [16384, 128], P(('row', 'col')), may hold values from -4 to 4
Outputs:
- grad_c: bfloat16 [16384, 512], P(('row', 'col'))
- grad_b: bfloat16 [16384, 128], P(('row', 'col'))
All inputs are finite; a program needn't handle non-finite values.
Results may differ from a plain program's by a relative error of at most 0.0056.
Values may be sent and summed in bfloat16 or wider, within the bound.
No kernel may reach another device: no remote copies, remote signals or barrier semaphores. Data moves between devices by JAX's collectives and lax.ppermute only.
A program may use at most 128 MiB of HBM per device.

v0:
```python
import math
import jax
import jax.numpy as jnp
from jax import lax
from jax.sharding import PartitionSpec as P

HEADS = 4
HEAD = 128
TOK_DEV = 128
LOSS_GAIN = 16.0
LENGTH_BASE = 512.0
NEGATIVE = -1e30


def teacher_logits(query_rows, key_rows, query_pos, key_pos):
    count = query_rows.shape[0]
    shaped = query_rows.reshape(count, HEADS, HEAD)
    logits = jnp.einsum("qhp,kp->hqk", shaped, key_rows, preferred_element_type=jnp.float32)
    temper = jnp.log(query_pos.astype(jnp.float32) + 2.0) / (
        math.log(LENGTH_BASE) * math.sqrt(HEAD)
    )
    logits = logits * temper[None, :, None]
    visible = key_pos[None, None, :] <= query_pos[None, :, None]
    return (jnp.where(visible, logits, NEGATIVE), visible)


def error_terms(logits, visible, peak, total, c_rows, b_rows, query_pos):
    probs = jnp.where(visible, jnp.exp(logits - peak[:, :, None]), 0.0) / total[:, :, None]
    count = c_rows.shape[0]
    shaped = c_rows.reshape(count, HEADS, HEAD)
    student = jnp.einsum("qhp,kp->hqk", shaped, b_rows, preferred_element_type=jnp.float32)
    student = student / (math.sqrt(HEAD) * (query_pos.astype(jnp.float32) + 1.0))[None, :, None]
    error = jnp.where(visible, student - probs, 0.0).astype(jnp.bfloat16)
    row_part = jnp.einsum("hqk,kp->qhp", error, b_rows, preferred_element_type=jnp.float32)
    key_part = jnp.einsum("hqk,qhp->kp", error, shaped, preferred_element_type=jnp.float32)
    return (row_part.reshape(count, HEADS * HEAD), key_part)


def on_device(hidden_states, w_c, w_b, teacher_q, teacher_k):
    c_proj = jnp.dot(hidden_states, w_c, preferred_element_type=jnp.float32).astype(jnp.bfloat16)
    b_proj = jnp.dot(hidden_states, w_b, preferred_element_type=jnp.float32).astype(jnp.bfloat16)
    key_rows, b_rows = (
        lax.all_gather(teacher_k, ("row", "col"), axis=0, tiled=True),
        lax.all_gather(b_proj, ("row", "col"), axis=0, tiled=True),
    )
    total_keys = key_rows.shape[0]
    width = math.gcd(2048, total_keys)
    turns = total_keys // width
    position_base = (lax.axis_index("row") * lax.axis_size("col") + lax.axis_index("col")) * TOK_DEV
    query_pos = position_base + jnp.arange(TOK_DEV, dtype=jnp.int32)
    key_split = key_rows.reshape(turns, width, HEAD)
    b_split = b_rows.reshape(turns, width, HEAD)
    pos_split = jnp.arange(total_keys, dtype=jnp.int32).reshape(turns, width)

    def stats_step(carry, pieces):
        logits, visible = teacher_logits(teacher_q, pieces[0], query_pos, pieces[1])
        newest = jnp.maximum(carry[0], jnp.max(logits, axis=2))
        summed = jnp.sum(jnp.where(visible, jnp.exp(logits - newest[:, :, None]), 0.0), axis=2)
        return ((newest, carry[1] * jnp.exp(carry[0] - newest) + summed), None)

    start_stats = (
        jnp.full((HEADS, TOK_DEV), NEGATIVE, jnp.float32),
        jnp.zeros((HEADS, TOK_DEV), jnp.float32),
    )
    (peak, total), unused = lax.scan(stats_step, start_stats, (key_split, pos_split))

    def rows_step(running, pieces):
        logits, visible = teacher_logits(teacher_q, pieces[0], query_pos, pieces[2])
        row_part, key_part = error_terms(logits, visible, peak, total, c_proj, pieces[1], query_pos)
        return (running + row_part, key_part)

    grad_rows, key_stack = lax.scan(
        rows_step, jnp.zeros((TOK_DEV, HEADS * HEAD), jnp.float32), (key_split, b_split, pos_split)
    )
    grad_keys = lax.psum_scatter(
        key_stack.reshape(total_keys, HEAD), ("row", "col"), scatter_dimension=0, tiled=True
    )
    factor = LOSS_GAIN / math.sqrt(HEAD)
    return ((grad_rows * factor).astype(jnp.bfloat16), (grad_keys * factor).astype(jnp.bfloat16))


def solution(mesh):
    return jax.shard_map(
        on_device,
        mesh=mesh,
        in_specs=(
            P(("row", "col"), None),
            P(),
            P(),
            P(("row", "col"), None),
            P(("row", "col"), None),
        ),
        out_specs=(P(("row", "col"), None), P(("row", "col"), None)),
        check_vma=False,
    )
```

profile of v0, /device:TPU:0, one launch (start us, length us, event | category | flops | bytes accessed | tf_op | source)
XLA Modules:
  0.0 1143.7 jit_solution(9247274924135349239)
XLA Ops:
  8.8 2.9 convolution_convert_fusion.1
  11.8 4.7 convolution_convert_fusion
  16.5 193.4 %all-gather.5.cloned.1.call-done = bf16[16384,128]{1,0:T(8,128)(2,1)} async-done(((bf16[128,128]{1,0:T(8,128)(2,1)}), bf16[16384,128]{1,0:T(8,128)(2,1)}) %all-gather.5.cloned.1.call-update) | async-done | bytes 4194320 | tf_op jit(solution)/shard_map/all_gather | solution.py:43
  210.0 58.9 %while.33 = (s32[]{:T(128)}, f32[4,128]{1,0:T(4,128)S(1)}, f32[4,128]{1,0:T(4,128)S(1)}, s32[8,2048]{1,0:T(8,128)S(1)}, bf16[8,2048,128]{2,1,0:T(8,128)(2,1)}, /...) while((s32[]{:T(128)}, f32[4,128]{1,0:T(4,128)S(1)}, ...), condition=%wide.region_3.4_spmd.clone.clone.clone, body=%wide.region_0.3_spmd.clone.clone.clone.sunk | while | flops 277089408 | bytes 9884788 | solution.py:65
  210.3 3.7 fusion.81
  214.0 3.2 select_reduce_fusion.2
  217.7 3.7 fusion.81
  221.4 3.2 select_reduce_fusion.2
  225.1 3.7 fusion.81
  228.8 3.2 select_reduce_fusion.2
  232.4 3.7 fusion.81
  236.2 3.2 select_reduce_fusion.2
  239.8 3.7 fusion.81
  243.5 3.2 select_reduce_fusion.2
  247.2 3.7 fusion.81
  250.9 3.2 select_reduce_fusion.2
  254.5 3.7 fusion.81
  258.2 3.2 select_reduce_fusion.2
  261.9 3.7 fusion.81
  265.6 3.2 select_reduce_fusion.2
  268.9 139.5 %all-gather.3.cloned.1.call-done = bf16[16384,128]{1,0:T(8,128)(2,1)} async-done(((bf16[128,128]{1,0:T(8,128)(2,1)}), bf16[16384,128]{1,0:T(8,128)(2,1)}) %all-gather.3.cloned.1.call-update) | async-done | bytes 4194320 | tf_op jit(solution)/shard_map/all_gather | solution.py:44
  408.3 66.1 %while.34 = (s32[]{:T(128)}, f32[128,512]{0,1:T(8,128)S(1)}, f32[8,2048,128]{2,1,0:T(8,128)}, bf16[8,2048,128]{2,1,0:T(8,128)(2,1)}, s32[8,2048]{1,0:T(8,128)S(1...) while((s32[]{:T(128)}, f32[128,512]{0,1:T(8,128)S(1)}, ...), condition=%wide.region_5.6_spmd.clone.clone.clone, body=%wide.region_4.5_spmd.clone.clone.clone.sunk | while | flops 1083573120 | bytes 19301524 | solution.py:72
  410.5 2.8 fusion.96
  418.7 2.8 fusion.96
  421.5 1.8 fusion.98
  427.0 2.8 fusion.96
  435.3 2.8 fusion.96
  443.5 2.8 fusion.96
  451.8 2.8 fusion.96
  460.0 2.8 fusion.96
  468.3 2.8 fusion.96
  475.2 660.4 %reduce-scatter.2.cloned.1.call-done = f32[128,128]{1,0:T(8,128)} async-done(((f32[16384,128]{1,0:T(8,128)}), f32[128,128]{1,0:T(8,128)}) %reduce-scatter.2.cloned.1.call-update) | async-done | bytes 65552 | tf_op jit(solution)/shard_map/reduce_scatter | solution.py:75
  (137 shorter events, 48.4 us)
Async XLA Ops:
  7.2 1.6 copy-start
  7.2 202.8 %all-gather.5.cloned.1.call-start = ((), (), s32[]{:S(2)}) async-start(), calls=%async_computation.2 | async-start | bytes 4227072 | tf_op jit(solution)/shard_map/all_gather | solution.py:43
  7.9 400.4 %all-gather.3.cloned.1.call-start = ((), (), s32[]{:S(2)}) async-start(), calls=%async_computation.1 | async-start | bytes 4227072 | tf_op jit(solution)/shard_map/all_gather | solution.py:44
  11.7 1124.0 %reduce-scatter.2.cloned.1.call-start = ((), (), s32[]{:S(2)}) async-start(), calls=%async_computation.3 | async-start | bytes 8454144 | tf_op jit(solution)/shard_map/reduce_scatter | solution.py:75
  11.8 198.2 %copy-start.1 = (bf16[128,512]{1,0:T(8,128)(2,1)S(1)}, bf16[128,512]{1,0:T(8,128)(2,1)}, u32[]{:S(2)}) copy-start(bf16[128,512]{1,0:T(8,128)(2,1)} %param.12) | copy-start | bytes 393220
Sparse Core Ops, SparseCore 0:
  9.7 200.2 all-gather.4
  212.3 196.0 all-gather.2
  474.6 661.0 reduce-scatter.1
where the time goes:
time: 1150 us; the launch traced here: 1140 us
  waiting for transfers between devices  994 us (86%)
  matrix products  99.3 us (9%)
  other arithmetic  34.2 us (3%)
  between operations  13.8 us (1%)
    reduce_scatter x1, waiting for transfers between devices, on_device(): lax.psum_scatter(key_stack.reshape(total_keys, HEAD), ('row', 'col'), sca...  660 us
    all_gather x1, waiting for transfers between devices, on_device(): lax.all_gather(teacher_k, ('row', 'col'), axis=0, tiled=True)  193 us
    all_gather x1, waiting for transfers between devices, on_device(): lax.all_gather(b_proj, ('row', 'col'), axis=0, tiled=True)  139 us
    dot_general x16, matrix products, teacher_logits(): jnp.einsum('qhp,kp->hqk', shaped, key_rows, preferred_element_type=jnp.fl...  51.9 us
    reduce_sum x8, other arithmetic, stats_step(): jnp.sum(jnp.where(visible, jnp.exp(logits - newest[:, :, None]), 0.0), ax...  25.8 us
  transfers between devices with their start and end apart: 3, of which 3 were waited for; matrix products, arithmetic and copies ran while one was open for 6% of the time, Pallas kernels for 0%

commit v1 on v0

--- a/solution.py
+++ b/solution.py
@@ -10,6 +10,11 @@
 LOSS_GAIN = 16.0
 LENGTH_BASE = 512.0
 NEGATIVE = -1e30
+
+
+def exchange_gather(x, axis, dim):
+    outgoing = jnp.stack([x] * lax.axis_size(axis))
+    return jnp.concatenate(lax.all_to_all(outgoing, axis, 0, 0), axis=dim)
 
 
 def teacher_logits(query_rows, key_rows, query_pos, key_pos):
@@ -40,7 +45,7 @@
     c_proj = jnp.dot(hidden_states, w_c, preferred_element_type=jnp.float32).astype(jnp.bfloat16)
     b_proj = jnp.dot(hidden_states, w_b, preferred_element_type=jnp.float32).astype(jnp.bfloat16)
     key_rows, b_rows = (
-        lax.all_gather(teacher_k, ("row", "col"), axis=0, tiled=True),
+        exchange_gather(teacher_k, ("row", "col"), 0),
         lax.all_gather(b_proj, ("row", "col"), axis=0, tiled=True),
     )
     total_keys = key_rows.shape[0]

time: 1150 us -> 986 us (0.86)
  waiting for transfers between devices: 994 us -> 819 us
  starting transfers between devices: 0.12 us -> 11.8 us
    all_gather x1 -> x0, waiting for transfers between devices: 193 us -> none  [on_device(): lax.all_gather(teacher_k, ('row', 'col'), axis=0, tiled=True)]
    all_to_all x0 -> x1, waiting for transfers between devices: none -> 45 us  [exchange_gather(): return jnp.concatenate(lax.all_to_all(outgoing, axis, 0, 0), axis=dim)]
    all_gather x1, waiting for transfers between devices: 139 us -> 112 us  [on_device(): lax.all_gather(b_proj, ('row', 'col'), axis=0, tiled=True)]
    all_to_all x0 -> x1, starting transfers between devices: none -> 11.7 us  [exchange_gather(): return jnp.concatenate(lax.all_to_all(outgoing, axis, 0, 0), axis=dim)]
  transfers between devices with their start and end apart: 3 -> 3, of which waited for: 3 -> 3; matrix products, arithmetic and copies ran while one was open for 6% -> 7% of each run, Pallas kernels for 0% -> 0%
where the time goes in v1:
time: 986 us; the launch traced here: 984 us
  waiting for transfers between devices  819 us (83%)
  matrix products  99.2 us (10%)
  other arithmetic  34.2 us (3%)
  between operations  14.1 us (1%)
  starting transfers between devices  11.8 us (1%)
    reduce_scatter x1, waiting for transfers between devices, on_device(): lax.psum_scatter(key_stack.reshape(total_keys, HEAD), ('row', 'col'), sca...  662 us
    all_gather x1, waiting for transfers between devices, on_device(): lax.all_gather(b_proj, ('row', 'col'), axis=0, tiled=True)  112 us
    dot_general x16, matrix products, teacher_logits(): jnp.einsum('qhp,kp->hqk', shaped, key_rows, preferred_element_type=jnp.fl...  51.8 us
    all_to_all x1, waiting for transfers between devices, exchange_gather(): return jnp.concatenate(lax.all_to_all(outgoing, axis, 0, 0), axis=dim)  45 us
    reduce_sum x8, other arithmetic, stats_step(): jnp.sum(jnp.where(visible, jnp.exp(logits - newest[:, :, None]), 0.0), ax...  25.8 us
  transfers between devices with their start and end apart: 3, of which 3 were waited for; matrix products, arithmetic and copies ran while one was open for 7% of the time, Pallas kernels for 0%

profile of v1, /device:TPU:0, one launch (start us, length us, event | category | flops | bytes accessed | tf_op | source)
XLA Modules:
  0.0 983.8 jit_solution(18238604275300601476)
XLA Ops:
  7.2 3.9 stack.2
  11.1 11.7 %all-to-all-start = ((bf16[128,128,128]{2,1,0:T(8,128)(2,1)}), bf16[128,128,128]{2,1,0:T(8,128)(2,1)}, u32[]{:S(2)}, u32[]{:S(2)}) async-start(bf16[128,128,128]{2,1,0:T(8,128)(2,1)} %stack.2), calls=%async_computation | async-start | bytes 8388608 | tf_op jit(solution)/shard_map/all_to_all | solution.py:17
  22.8 2.9 convolution_convert_fusion.1
  25.9 4.7 convolution_convert_fusion
  30.6 45.0 %all-to-all-done = bf16[128,128,128]{2,1,0:T(8,128)(2,1)} async-done(((bf16[128,128,128]{2,1,0:T(8,128)(2,1)}), bf16[128,128,128]{2,1,0:T(8,128)(2,1)}, u32[]{:S(2)}, u32[]{:S(2)}) %all-to-all-start) | async-done | bytes 4194336 | tf_op jit(solution)/shard_map/all_to_all | solution.py:17
  75.6 58.8 %while.33 = (s32[]{:T(128)}, f32[4,128]{1,0:T(4,128)S(1)}, f32[4,128]{1,0:T(4,128)S(1)}, s32[8,2048]{1,0:T(8,128)S(1)}, bf16[8,2048,128]{2,1,0:T(8,128)(2,1)}, /...) while((s32[]{:T(128)}, f32[4,128]{1,0:T(4,128)S(1)}, ...), condition=%wide.region_3.4_spmd.clone.clone.clone, body=%wide.region_0.3_spmd.clone.clone.clone.sunk | while | flops 277089408 | bytes 9884788 | solution.py:70
  76.0 3.7 fusion.81
  79.7 3.2 select_reduce_fusion.2
  83.4 3.7 fusion.81
  87.1 3.2 select_reduce_fusion.2
  90.7 3.7 fusion.81
  94.4 3.2 select_reduce_fusion.2
  98.1 3.7 fusion.81
  101.8 3.2 select_reduce_fusion.2
  105.4 3.7 fusion.81
  109.1 3.2 select_reduce_fusion.2
  112.8 3.7 fusion.81
  116.5 3.2 select_reduce_fusion.2
  120.1 3.7 fusion.81
  123.8 3.2 select_reduce_fusion.2
  127.5 3.7 fusion.81
  131.2 3.2 select_reduce_fusion.2
  134.5 112.2 %all-gather.2.cloned.1.call-done = bf16[16384,128]{1,0:T(8,128)(2,1)} async-done(((bf16[128,128]{1,0:T(8,128)(2,1)}), bf16[16384,128]{1,0:T(8,128)(2,1)}) %all-gather.2.cloned.1.call-update) | async-done | bytes 4194320 | tf_op jit(solution)/shard_map/all_gather | solution.py:49
  246.6 66.0 %while.34 = (s32[]{:T(128)}, f32[128,512]{0,1:T(8,128)S(1)}, f32[8,2048,128]{2,1,0:T(8,128)}, bf16[8,2048,128]{2,1,0:T(8,128)(2,1)}, s32[8,2048]{1,0:T(8,128)S(1...) while((s32[]{:T(128)}, f32[128,512]{0,1:T(8,128)S(1)}, ...), condition=%wide.region_5.6_spmd.clone.clone.clone, body=%wide.region_4.5_spmd.clone.clone.clone.sunk | while | flops 1083573120 | bytes 19301524 | solution.py:77
  248.8 2.8 fusion.96
  257.0 2.8 fusion.96
  265.3 2.8 fusion.96
  273.5 2.8 fusion.96
  281.8 2.8 fusion.96
  290.0 2.8 fusion.96
  298.3 2.8 fusion.96
  313.5 662.0 %reduce-scatter.2.cloned.1.call-done = f32[128,128]{1,0:T(8,128)} async-done(((f32[16384,128]{1,0:T(8,128)}), f32[128,128]{1,0:T(8,128)}) %reduce-scatter.2.cloned.1.call-update) | async-done | bytes 65552 | tf_op jit(solution)/shard_map/reduce_scatter | solution.py:80
  (137 shorter events, 51.4 us)
Async XLA Ops:
  7.2 15.7 %copy-start = (bf16[128,8192]{1,0:T(8,128)(2,1)S(1)}, bf16[128,8192]{1,0:T(8,128)(2,1)}, u32[]{:S(2)}) copy-start(bf16[128,8192]{1,0:T(8,128)(2,1)} %param.9) | copy-start | bytes 6291460
  11.1 64.5 %all-to-all-start = ((bf16[128,128,128]{2,1,0:T(8,128)(2,1)}), bf16[128,128,128]{2,1,0:T(8,128)(2,1)}, u32[]{:S(2)}, u32[]{:S(2)}) async-start(bf16[128,128,128]{2,1,0:T(8,128)(2,1)} %stack.2), calls=%async_computation | async-start | bytes 8388608 | tf_op jit(solution)/shard_map/all_to_all | solution.py:17
  22.8 223.9 %all-gather.2.cloned.1.call-start = ((), (), s32[]{:S(2)}) async-start(), calls=%async_computation.2 | async-start | bytes 4227072 | tf_op jit(solution)/shard_map/all_gather | solution.py:49
  25.8 949.8 %reduce-scatter.2.cloned.1.call-start = ((), (), s32[]{:S(2)}) async-start(), calls=%async_computation.3 | async-start | bytes 8454144 | tf_op jit(solution)/shard_map/reduce_scatter | solution.py:80
  25.9 49.7 %copy-start.1 = (bf16[128,512]{1,0:T(8,128)(2,1)S(1)}, bf16[128,512]{1,0:T(8,128)(2,1)}, u32[]{:S(2)}) copy-start(bf16[128,512]{1,0:T(8,128)(2,1)} %param.12) | copy-start | bytes 393220
Sparse Core Ops, SparseCore 0:
  25.9 220.7 all-gather.1
  312.8 662.6 reduce-scatter.1

commit v2 on v0

--- a/solution.py
+++ b/solution.py
@@ -10,6 +10,11 @@
 LOSS_GAIN = 16.0
 LENGTH_BASE = 512.0
 NEGATIVE = -1e30
+
+
+def swapped_in(x, axis, along):
+    repeated = jnp.stack([x] * lax.axis_size(axis))
+    return jnp.concatenate(lax.all_to_all(repeated, axis, 0, 0), axis=along)
 
 
 def teacher_logits(query_rows, key_rows, query_pos, key_pos):
@@ -41,7 +46,7 @@
     b_proj = jnp.dot(hidden_states, w_b, preferred_element_type=jnp.float32).astype(jnp.bfloat16)
     key_rows, b_rows = (
         lax.all_gather(teacher_k, ("row", "col"), axis=0, tiled=True),
-        lax.all_gather(b_proj, ("row", "col"), axis=0, tiled=True),
+        swapped_in(b_proj, ("row", "col"), 0),
     )
     total_keys = key_rows.shape[0]
     width = math.gcd(2048, total_keys)

time: 1150 us -> 1040 us (0.904)
  waiting for transfers between devices: 994 us -> 873 us
  starting transfers between devices: 0.12 us -> 11.8 us
    all_gather x1 -> x0, waiting for transfers between devices: 139 us -> none  [on_device(): lax.all_gather(b_proj, ('row', 'col'), axis=0, tiled=True)]
    all_gather x1, waiting for transfers between devices: 193 us -> 212 us  [on_device(): lax.all_gather(teacher_k, ('row', 'col'), axis=0, tiled=True)]
    all_to_all x0 -> x1, starting transfers between devices: none -> 11.7 us  [swapped_in(): return jnp.concatenate(lax.all_to_all(repeated, axis, 0, 0), axis=along)]
  transfers between devices with their start and end apart: 3 -> 3, of which waited for: 3 -> 2; matrix products, arithmetic and copies ran while one was open for 6% -> 7% of each run, Pallas kernels for 0% -> 0%
where the time goes in v2:
time: 1040 us
  waiting for transfers between devices  873 us (84%)
  matrix products  98.9 us (10%)
  other arithmetic  34.2 us (3%)
  between operations  14.1 us (1%)
  starting transfers between devices  11.8 us (1%)
    reduce_scatter x1, waiting for transfers between devices, on_device(): lax.psum_scatter(key_stack.reshape(total_keys, HEAD), ('row', 'col'), sca...  660 us
    all_gather x1, waiting for transfers between devices, on_device(): lax.all_gather(teacher_k, ('row', 'col'), axis=0, tiled=True)  212 us
    dot_general x16, matrix products, teacher_logits(): jnp.einsum('qhp,kp->hqk', shaped, key_rows, preferred_element_type=jnp.fl...  52.2 us
    reduce_sum x8, other arithmetic, stats_step(): jnp.sum(jnp.where(visible, jnp.exp(logits - newest[:, :, None]), 0.0), ax...  25.8 us
  transfers between devices with their start and end apart: 3, of which 2 were waited for; matrix products, arithmetic and copies ran while one was open for 7% of the time, Pallas kernels for 0%

profile of v2, /device:TPU:0, one launch (start us, length us, event | category | flops | bytes accessed | tf_op | source)
XLA Modules:
  0.0 1037.5 jit_solution(8084593693383737608)
XLA Ops:
  8.8 2.3 convolution_convert_fusion.1
  11.1 3.0 stack.2
  14.0 11.7 %all-to-all-start = ((bf16[128,128,128]{2,1,0:T(8,128)(2,1)}), bf16[128,128,128]{2,1,0:T(8,128)(2,1)}, u32[]{:S(2)}, u32[]{:S(2)}) async-start(bf16[128,128,128]{2,1,0:T(8,128)(2,1)} %stack.2), calls=%async_computation | async-start | bytes 8388608 | tf_op jit(solution)/shard_map/all_to_all | solution.py:17
  25.9 4.7 convolution_convert_fusion
  30.6 212.3 %all-gather.2.cloned.1.call-done = bf16[16384,128]{1,0:T(8,128)(2,1)} async-done(((bf16[128,128]{1,0:T(8,128)(2,1)}), bf16[16384,128]{1,0:T(8,128)(2,1)}) %all-gather.2.cloned.1.call-update) | async-done | bytes 4194320 | tf_op jit(solution)/shard_map/all_gather | solution.py:48
  242.9 59.1 %while.33 = (s32[]{:T(128)}, f32[4,128]{1,0:T(4,128)S(1)}, f32[4,128]{1,0:T(4,128)S(1)}, s32[8,2048]{1,0:T(8,128)S(1)}, bf16[8,2048,128]{2,1,0:T(8,128)(2,1)}, /...) while((s32[]{:T(128)}, f32[4,128]{1,0:T(4,128)S(1)}, ...), condition=%wide.region_3.4_spmd.clone.clone.clone, body=%wide.region_0.3_spmd.clone.clone.clone.sunk | while | flops 277089408 | bytes 9884788 | solution.py:70
  243.2 3.7 fusion.81
  247.0 3.2 select_reduce_fusion.2
  250.6 3.7 fusion.81
  254.4 3.2 select_reduce_fusion.2
  258.0 3.7 fusion.81
  261.8 3.2 select_reduce_fusion.2
  265.4 3.7 fusion.81
  269.2 3.2 select_reduce_fusion.2
  272.8 3.7 fusion.81
  276.6 3.2 select_reduce_fusion.2
  280.2 3.7 fusion.81
  283.9 3.2 select_reduce_fusion.2
  287.6 3.7 fusion.81
  291.3 3.2 select_reduce_fusion.2
  295.0 3.7 fusion.81
  298.7 3.2 select_reduce_fusion.2
  302.0 66.0 %while.34 = (s32[]{:T(128)}, f32[128,512]{0,1:T(8,128)S(1)}, f32[8,2048,128]{2,1,0:T(8,128)}, bf16[8,2048,128]{2,1,0:T(8,128)(2,1)}, s32[8,2048]{1,0:T(8,128)S(1...) while((s32[]{:T(128)}, f32[128,512]{0,1:T(8,128)S(1)}, ...), condition=%wide.region_5.6_spmd.clone.clone.clone, body=%wide.region_4.5_spmd.clone.clone.clone.sunk | while | flops 1083573120 | bytes 19301524 | solution.py:77
  304.1 2.8 fusion.96
  312.4 2.8 fusion.96
  320.7 2.8 fusion.96
  328.9 2.8 fusion.96
  337.2 2.8 fusion.96
  345.4 2.8 fusion.96
  353.7 2.8 fusion.96
  361.9 2.8 fusion.96
  368.9 660.3 %reduce-scatter.2.cloned.1.call-done = f32[128,128]{1,0:T(8,128)} async-done(((f32[16384,128]{1,0:T(8,128)}), f32[128,128]{1,0:T(8,128)}) %reduce-scatter.2.cloned.1.call-update) | async-done | bytes 65552 | tf_op jit(solution)/shard_map/reduce_scatter | solution.py:80
  (137 shorter events, 50.1 us)
Async XLA Ops:
  7.2 1.6 copy-start
  7.2 235.7 %all-gather.2.cloned.1.call-start = ((), (), s32[]{:S(2)}) async-start(), calls=%async_computation.2 | async-start | bytes 4227072 | tf_op jit(solution)/shard_map/all_gather | solution.py:48
  14.0 288.0 %all-to-all-start = ((bf16[128,128,128]{2,1,0:T(8,128)(2,1)}), bf16[128,128,128]{2,1,0:T(8,128)(2,1)}, u32[]{:S(2)}, u32[]{:S(2)}) async-start(bf16[128,128,128]{2,1,0:T(8,128)(2,1)} %stack.2), calls=%async_computation | async-start | bytes 8388608 | tf_op jit(solution)/shard_map/all_to_all | solution.py:17
  25.7 1003.5 %reduce-scatter.2.cloned.1.call-start = ((), (), s32[]{:S(2)}) async-start(), calls=%async_computation.3 | async-start | bytes 8454144 | tf_op jit(solution)/shard_map/reduce_scatter | solution.py:80
  25.9 217.0 %copy-start.1 = (bf16[128,512]{1,0:T(8,128)(2,1)S(1)}, bf16[128,512]{1,0:T(8,128)(2,1)}, u32[]{:S(2)}) copy-start(bf16[128,512]{1,0:T(8,128)(2,1)} %param.12) | copy-start | bytes 393220
Sparse Core Ops, SparseCore 0:
  9.7 233.0 all-gather.1
  368.2 660.9 reduce-scatter.1
